TPU v7x, 128 devices: a whole 4x4x4 slice. The times are simulated.
128 devices in a mesh: row: 16 (over y, x), col: 4 (over z), depth: 2 (over core).
Axes of the slice: x: 4, y: 4, z: 4, core: 2. Of those that a mesh axis runs over, the one named last changes fastest.
Arguments:
- layers: float32 [2, 16384, 16384], P('depth', 'row', 'col'), may hold values from -3 to 265.4, as said below
Outputs:
- factor: float32 [2, 16384, 512], P(None, 'row', 'depth')
- schur: float32 [16384, 16384], P(('row', 'depth'), 'col')
Inputs may be any that keep to these rules, and one draw needn't show every extreme that they name: Read in matrix order, each layer is symmetric, and the sum over layers is symmetric positive definite with a diagonal of order sqrt(16384).
All inputs are finite; a program needn't handle non-finite values.
Results may differ from a plain program's by a relative error of at most 0.0001.
Values sent between devices are 32-bit elements; how exact they have to be, the bound alone decides.
No kernel may reach another device: no remote copies, remote signals or barrier semaphores. Data moves between devices by JAX's collectives and lax.ppermute only.
A program may use at most 192 MiB of HBM per device.

v0:
```python
import jax
import jax.numpy as jnp
from jax import lax
from jax.sharding import PartitionSpec as P

PANEL = 512
PANELS = 2


def broadcast(value, axis, source):
    kept = jnp.where(lax.axis_index(axis) == source, value, 0).astype(value.dtype)
    return lax.psum(kept, axis)


def sent_to_all(x, axis):
    devices = lax.axis_size(axis)
    return lax.all_to_all(jnp.broadcast_to(x[None], (devices, *x.shape)), axis, 0, 0, tiled=True)


def of_everyone(x, axis):
    return sent_to_all(x, axis).sum(axis=0)


def cut_along(x, dim, devices):
    before, after = (x.shape[:dim], x.shape[dim + 1 :])
    return jnp.moveaxis(x.reshape(*before, devices, -1, *after), dim, 0)


def summed_on_arrival(x, axis, dim):
    devices = lax.axis_size(axis)
    tiles = lax.all_to_all(cut_along(x, dim, devices), axis, 0, 0, tiled=True)
    return jnp.sum(tiles, axis=0)


def broadcast_2(x, axis, root):
    return lax.dynamic_index_in_dim(lax.all_gather(x, axis), root, 0, keepdims=False)


def block_inverse(diagonal, identity_block):
    lower_diag = jnp.linalg.cholesky(diagonal)
    return jax.scipy.linalg.solve_triangular(lower_diag, identity_block, lower=True)


def outer_update(left_rows, right_rows):
    return lax.dot_general(
        left_rows,
        right_rows,
        (((1,), (1,)), ((), ())),
        precision=lax.Precision.HIGHEST,
        preferred_element_type=jnp.float32,
    )


def per_device(layers):
    row_groups = lax.axis_size("row")
    col_groups = lax.axis_size("col")
    depth_groups = lax.axis_size("depth")
    row_index = lax.axis_index("row")
    col_index = lax.axis_index("col")
    depth_index = lax.axis_index("depth")
    layer_part = layers[0]
    rows_local = layer_part.shape[0]
    cols_local = layer_part.shape[1]
    slice_width = PANEL // depth_groups
    quarter_rows = rows_local // depth_groups
    local_blocks = rows_local // PANEL
    row_block = jnp.arange(rows_local, dtype=jnp.int32) // PANEL * row_groups + row_index
    col_block = jnp.arange(cols_local, dtype=jnp.int32) // PANEL * col_groups + col_index
    identity_block = jnp.eye(PANEL, dtype=jnp.float32)
    factor_list = []
    schur = None
    for panel_step in range(PANELS):
        owner_col = panel_step % col_groups
        local_col = panel_step // col_groups
        owner_row = panel_step % row_groups
        local_row = panel_step // row_groups
        column = layer_part[:, local_col * PANEL : (local_col + 1) * PANEL]
        layer_diag = broadcast(
            column[local_row * PANEL : (local_row + 1) * PANEL], "row", owner_row
        )
        diagonal = of_everyone(layer_diag, "depth")
        quarter = summed_on_arrival(column, "depth", 0)
        inverse = block_inverse(diagonal, identity_block)
        solved = jnp.dot(quarter, inverse.T, precision=lax.Precision.HIGHEST)
        quarter_block = lax.dynamic_slice_in_dim(
            row_block, depth_index * quarter_rows, quarter_rows, 0
        )
        solved = jnp.where(quarter_block[:, None] >= panel_step, solved, 0.0)
        row_slice = lax.all_to_all(solved, "depth", split_axis=1, concat_axis=0, tiled=True)
        panel_rows = broadcast_2(row_slice, "col", owner_col)
        factor_list.append(panel_rows)
        update_rows = jnp.where(row_block[:, None] > panel_step, panel_rows, 0.0)
        gathered = lax.all_gather(panel_rows, "row", axis=0, tiled=True)
        grouped = gathered.reshape(
            row_groups // col_groups, col_groups, local_blocks, PANEL, slice_width
        )
        picked = lax.dynamic_index_in_dim(grouped, col_index, 1, keepdims=False)
        column_rows = picked.transpose(1, 0, 2, 3).reshape(cols_local, slice_width)
        update_cols = jnp.where(col_block[:, None] > panel_step, column_rows, 0.0)
        if panel_step + 1 < PANELS:
            layer_part = layer_part - outer_update(update_rows, update_cols)
        else:
            schur = summed_on_arrival(
                layer_part - outer_update(update_rows, update_cols), "depth", 0
            )
    return (jnp.stack(factor_list), schur)


def solution(mesh):
    return jax.shard_map(
        per_device,
        mesh=mesh,
        in_specs=(P("depth", "row", "col"),),
        out_specs=(P(None, "row", "depth"), P(("row", "depth"), "col")),
        check_vma=False,
    )
```

profile of v0, /device:TPU:1, one launch (start us, length us, event | category | flops | bytes accessed | tf_op | source)
XLA Modules:
  0.0 959.5 jit_solution(3367410215411466751)
XLA Ops:
  7.2 17.5 %copy.41 = f32[1,1024,4096]{1,2,0:T(8,128)} copy(f32[1,1024,4096]{2,1,0:T(8,128)} %param.4) | data formatting | bytes 33554432 | tf_op args[0]
  24.7 2.3 slice_select_fusion.1
  27.0 1.7 slice.113
  28.7 1.5 copy.80
  30.2 5.1 all-to-all-start
  35.4 2.5 all-to-all-done
  39.3 76.7 %all-reduce.4.cloned.1.call-done = f32[512,512]{0,1:T(8,128)} async-done(((f32[512,512]{0,1:T(8,128)}), f32[512,512]{0,1:T(8,128)}) %all-reduce.4.cloned.1.call-update) | async-done | bytes 1048592 | tf_op jit(solution)/shard_map/psum | solution.py:12
  116.0 1.6 copy.44
  117.8 8.2 all_to_all.57
  126.0 1.9 reduce_sum.46
  129.4 11.7 %cholesky.286 = f32[128,128]{1,0:T(8,128)S(1)} custom-call(f32[128,128]{1,0:T(8,128)S(1)} %cholesky.426), custom_call_target="Cholesky" | custom-call | tf_op jit(solution)/shard_map/jit(cholesky)/cholesky | solution.py:40
  141.2 9.8 %custom-call.27 = f32[1,128,128]{1,2,0:T(8,128)S(1)} custom-call(f32[1,128,128]{2,1,0:T(8,128)S(1)} %get-tuple-element.63), custom_call_target="InvertDiagBlocksLowerTriangular" | custom-call | tf_op jit(solution)/shard_map/jit(cholesky)/cholesky | solution.py:40
  153.6 11.7 %cholesky.305 = f32[128,128]{1,0:T(8,128)S(1)} custom-call(f32[128,128]{1,0:T(8,128)S(1)} %cholesky.430), custom_call_target="Cholesky" | custom-call | tf_op jit(solution)/shard_map/jit(cholesky)/cholesky | solution.py:40
  165.4 10.1 %custom-call.28 = f32[1,128,128]{1,2,0:T(8,128)S(1)} custom-call(f32[1,128,128]{2,1,0:T(8,128)S(1)} %get-tuple-element.60), custom_call_target="InvertDiagBlocksLowerTriangular" | custom-call | tf_op jit(solution)/shard_map/jit(cholesky)/cholesky | solution.py:40
  177.1 11.7 %cholesky.326 = f32[128,128]{1,0:T(8,128)S(1)} custom-call(f32[128,128]{1,0:T(8,128)S(1)} %cholesky.435), custom_call_target="Cholesky" | custom-call | tf_op jit(solution)/shard_map/jit(cholesky)/cholesky | solution.py:40
  189.5 9.8 %custom-call.29 = f32[1,128,128]{1,2,0:T(8,128)S(1)} custom-call(f32[1,128,128]{2,1,0:T(8,128)S(1)} %get-tuple-element.57), custom_call_target="InvertDiagBlocksLowerTriangular" | custom-call | tf_op jit(solution)/shard_map/jit(cholesky)/cholesky | solution.py:40
  200.7 11.9 %cholesky.343 = f32[128,128]{1,0:T(8,128)S(1)} custom-call(f32[128,128]{1,0:T(8,128)S(1)} %convolution_subtract_fusion.13), custom_call_target="Cholesky" | custom-call | tf_op jit(solution)/shard_map/jit(cholesky)/cholesky | solution.py:40
  217.7 11.7 %while.4 = (s32[]{:T(128)}, f32[512,512]{1,0:T(8,128)}, s32[4,2]{0,1:T(2,128)S(1)}, f32[4,128,128]{2,1,0:T(8,128)S(1)}, s32[]{:T(128)}) while((s32[]{:T(128)}, f32[512,512]{1,0:T(8,128)}, s32[4,2]{0,1:T(2,128)S(1)}, f32[4,128,128]{2,1,0:T(8,128)S(1)}, s32[]{:T(128)}) %tuple.58), condition=%wide.while_cond, body=%wide.while_body.sunk | while | flops 2 | bytes 131181 | solution.py:41
  218.3 2.2 bitcast_dynamic-update-slice_fusion.4
  221.3 2.2 bitcast_dynamic-update-slice_fusion.4
  224.2 2.2 bitcast_dynamic-update-slice_fusion.4
  227.2 2.2 bitcast_dynamic-update-slice_fusion.4
  229.3 39.3 %custom-call.30 = f32[4,128,128]{1,2,0:T(8,128)S(1)} custom-call(f32[4,128,128]{2,1,0:T(8,128)S(1)} %get-tuple-element.18), custom_call_target="InvertDiagBlocksLowerTriangular" | custom-call | tf_op jit(solution)/shard_map/jit(_solve_triangular)/triangular_solve | solution.py:41
  270.7 1.3 convolution_subtract_fusion.4
  272.5 1.6 convolution_subtract_fusion.7
  274.5 1.9 convolution_select_fusion.1
  276.4 4.6 all_to_all.58
  282.4 47.3 %all-gather.7.cloned.1.call-done = f32[4,1024,256]{2,1,0:T(8,128)} async-done(((f32[1,1024,256]{2,1,0:T(8,128)}), f32[4,1024,256]{2,1,0:T(8,128)}) %all-gather.7.cloned.1.call-update) | async-done | bytes 4194320 | tf_op jit(solution)/shard_map/all_gather | solution.py:36
  329.7 2.3 dynamic_slice.23
  332.1 111.6 %all-gather.11.cloned.1.call-done = f32[1,16384,256]{2,1,0:T(8,128)} async-done(((f32[1,1024,256]{2,1,0:T(8,128)}), f32[1,16384,256]{2,1,0:T(8,128)}) %all-gather.11.cloned.1.call-update) | async-done | bytes 16777232 | tf_op jit(solution)/shard_map/all_gather | solution.py:93
  443.7 3.3 fusion.1
  446.9 19.2 %convolution_subtract_fusion.1 = f32[1024,4096]{0,1:T(8,128)} fusion(f32[4096,256]{1,0:T(8,128)S(1)} %bitcast.148, pred[1024]{0:T(1024)(128)(4,1)S(1)} %broadcast_compare_fusion.2, f32[1,1024,4096]{1,2,0:T(8,128)} %copy.41, f32[4,1024,256]{2,1,0:T(8,128)} %all-gather.7.cloned.1.call-done), kind=kOutput, calls=%fused_computation.6 | convolution fusion | flops 12889358336 | bytes 38798336 | tf_op jit(solution)/shard_map/dot_general | solution.py:45
  466.1 2.5 slice_select_fusion
  468.9 5.9 all_to_all.59
  476.0 78.3 %all-reduce.6.cloned.1.call-done = f32[512,512]{0,1:T(8,128)} async-done(((f32[512,512]{0,1:T(8,128)}), f32[512,512]{0,1:T(8,128)}) %all-reduce.6.cloned.1.call-update) | async-done | bytes 1048592 | tf_op jit(solution)/shard_map/psum | solution.py:12
  554.3 1.6 copy.51
  556.1 8.2 all_to_all.60
  564.2 1.9 reduce_sum.48
  567.7 11.7 %cholesky.358 = f32[128,128]{1,0:T(8,128)S(1)} custom-call(f32[128,128]{1,0:T(8,128)S(1)} %cholesky.439), custom_call_target="Cholesky" | custom-call | tf_op jit(solution)/shard_map/jit(cholesky)/cholesky | solution.py:40
  579.6 9.8 %custom-call.31 = f32[1,128,128]{1,2,0:T(8,128)S(1)} custom-call(f32[1,128,128]{2,1,0:T(8,128)S(1)} %get-tuple-element.53), custom_call_target="InvertDiagBlocksLowerTriangular" | custom-call | tf_op jit(solution)/shard_map/jit(cholesky)/cholesky | solution.py:40
  591.9 11.7 %cholesky.377 = f32[128,128]{1,0:T(8,128)S(1)} custom-call(f32[128,128]{1,0:T(8,128)S(1)} %cholesky.443), custom_call_target="Cholesky" | custom-call | tf_op jit(solution)/shard_map/jit(cholesky)/cholesky | solution.py:40
  605.0 10.0 %custom-call.32 = f32[1,128,128]{1,2,0:T(8,128)S(1)} custom-call(f32[1,128,128]{2,1,0:T(8,128)S(1)} %get-tuple-element.50), custom_call_target="InvertDiagBlocksLowerTriangular" | custom-call | tf_op jit(solution)/shard_map/jit(cholesky)/cholesky | solution.py:40
  616.6 11.7 %cholesky.398 = f32[128,128]{1,0:T(8,128)S(1)} custom-call(f32[128,128]{1,0:T(8,128)S(1)} %cholesky.448), custom_call_target="Cholesky" | custom-call | tf_op jit(solution)/shard_map/jit(cholesky)/cholesky | solution.py:40
  629.0 9.8 %custom-call.33 = f32[1,128,128]{1,2,0:T(8,128)S(1)} custom-call(f32[1,128,128]{2,1,0:T(8,128)S(1)} %get-tuple-element.47), custom_call_target="InvertDiagBlocksLowerTriangular" | custom-call | tf_op jit(solution)/shard_map/jit(cholesky)/cholesky | solution.py:40
  640.3 11.9 %cholesky.415 = f32[128,128]{1,0:T(8,128)S(1)} custom-call(f32[128,128]{1,0:T(8,128)S(1)} %convolution_subtract_fusion.12), custom_call_target="Cholesky" | custom-call | tf_op jit(solution)/shard_map/jit(cholesky)/cholesky | solution.py:40
  656.4 11.7 %while.5 = (s32[]{:T(128)}, f32[512,512]{1,0:T(8,128)}, s32[4,2]{0,1:T(2,128)S(1)}, f32[4,128,128]{2,1,0:T(8,128)S(1)}, s32[]{:T(128)}) while((s32[]{:T(128)}, f32[512,512]{1,0:T(8,128)}, s32[4,2]{0,1:T(2,128)S(1)}, f32[4,128,128]{2,1,0:T(8,128)S(1)}, s32[]{:T(128)}) %tuple.76), condition=%wide.while_cond.clone, body=%wide.while_body.clone.sunk | while | flops 2 | bytes 131181 | solution.py:41
  657.1 2.2 bitcast_dynamic-update-slice_fusion.5
  660.1 2.2 bitcast_dynamic-update-slice_fusion.5
  663.0 2.2 bitcast_dynamic-update-slice_fusion.5
  665.9 2.2 bitcast_dynamic-update-slice_fusion.5
  668.1 39.3 %custom-call.34 = f32[4,128,128]{1,2,0:T(8,128)S(1)} custom-call(f32[4,128,128]{2,1,0:T(8,128)S(1)} %get-tuple-element.19), custom_call_target="InvertDiagBlocksLowerTriangular" | custom-call | tf_op jit(solution)/shard_map/jit(_solve_triangular)/triangular_solve | solution.py:41
  711.3 1.6 convolution_subtract_fusion.6
  713.3 1.9 convolution_select_fusion
  715.2 4.7 all_to_all.61
  721.3 47.3 %all-gather.9.cloned.1.call-done = f32[4,1024,256]{2,1,0:T(8,128)} async-done(((f32[1,1024,256]{2,1,0:T(8,128)}), f32[4,1024,256]{2,1,0:T(8,128)}) %all-gather.9.cloned.1.call-update) | async-done | bytes 4194320 | tf_op jit(solution)/shard_map/all_gather | solution.py:36
  768.6 2.3 dynamic_slice.24
  770.9 2.7 pad_maximum_fusion
  773.6 108.8 %all-gather.13.cloned.1.call-done = f32[1,16384,256]{2,1,0:T(8,128)} async-done(((f32[1,1024,256]{2,1,0:T(8,128)}), f32[1,16384,256]{2,1,0:T(8,128)}) %all-gather.13.cloned.1.call-update) | async-done | bytes 16777232 | tf_op jit(solution)/shard_map/all_gather | solution.py:93
  882.4 3.5 fusion
  885.9 19.2 %convolution_subtract_fusion = f32[1024,4096]{0,1:T(8,128)} fusion(f32[1024,4096]{0,1:T(8,128)} %convolution_subtract_fusion.1, f32[4096,256]{1,0:T(8,128)S(1)} %bitcast.147, pred[1024]{0:T(1024)(128)(4,1)S(1)} %broadcast_compare_fusion.3, f32[4,1024,256]{2,1,0:T(8,128)} %all-gather.9.cloned.1.call-done), kind=kOutput, calls=%fused_computation.5 | convolution fusion | flops 12889358336 | bytes 38798336 | tf_op jit(solution)/shard_map/dot_general | solution.py:45
  905.1 6.8 copy.78
  911.9 19.5 %all_to_all.62 = f32[2,512,4096]{1,2,0:T(8,128)} all-to-all(f32[2,512,4096]{1,2,0:T(8,128)S(1)} %bitcast.146), channel_id=1, replica_groups=mesh['row'=16,'col'=4,'depth'=2] {'depth'}, dimensions={0} | all-to-all | bytes 33554432 | tf_op jit(solution)/shard_map/all_to_all | solution.py:31
  931.4 11.9 %reduce_sum.49 = f32[512,4096]{0,1:T(8,128)} reduce(f32[2,512,4096]{1,2,0:T(8,128)} %all_to_all.62, f32[]{:T(128)} %constant.194.clone.1), dimensions={0}, to_apply=%region_14.17 | reduce | flops 2097152 | bytes 25165828 | tf_op jit(solution)/shard_map/reduce_sum | solution.py:32
  943.3 8.9 copy.58
  (110 shorter events, 40.3 us)
Async XLA Ops:
  7.2 108.8 %all-reduce.4.cloned.1.call-start = ((), (), s32[]{:S(2)}) async-start(), calls=%async_computation.7 | async-start | bytes 2097152 | tf_op jit(solution)/shard_map/psum | solution.py:12
  30.2 7.6 all-to-all-start
  35.4 294.3 %all-gather.7.cloned.1.call-start = ((), (), s32[]{:S(2)}) async-start(), calls=%async_computation.8 | async-start | bytes 5242880 | tf_op jit(solution)/shard_map/all_gather | solution.py:36
  128.4 1.0 copy-start.4
  216.5 58.0 %copy-start.1 = (f32[512,512]{0,1:T(8,128)S(1)}, f32[512,512]{0,1:T(8,128)}, u32[]{:S(2)}) copy-start(f32[512,512]{0,1:T(8,128)} %reduce_sum.45) | copy-start | bytes 3145732
  282.3 161.3 %all-gather.11.cloned.1.call-start = ((), (), s32[]{:S(2)}) async-start(), calls=%async_computation.11 | async-start | bytes 17825792 | tf_op jit(solution)/shard_map/all_gather | solution.py:93
  331.9 222.3 %all-reduce.6.cloned.1.call-start = ((), (), s32[]{:S(2)}) async-start(), calls=%async_computation.9 | async-start | bytes 2097152 | tf_op jit(solution)/shard_map/psum | solution.py:12
  466.1 2.6 slice-start
  468.6 300.0 %all-gather.9.cloned.1.call-start = ((), (), s32[]{:S(2)}) async-start(), calls=%async_computation.10 | async-start | bytes 5242880 | tf_op jit(solution)/shard_map/all_gather | solution.py:36
  566.7 1.0 copy-start.3
  655.3 58.0 %copy-start.2 = (f32[512,512]{0,1:T(8,128)S(1)}, f32[512,512]{0,1:T(8,128)}, u32[]{:S(2)}) copy-start(f32[512,512]{0,1:T(8,128)} %reduce_sum.47) | copy-start | bytes 3145732
  715.2 55.7 %copy-start = (f32[1,1024,256]{2,1,0:T(8,128)S(1)}, f32[1,1024,256]{2,1,0:T(8,128)}, u32[]{:S(2)}) copy-start(f32[1,1024,256]{2,1,0:T(8,128)} %dynamic_slice.23) | copy-start | bytes 3145732
  721.2 161.2 %all-gather.13.cloned.1.call-start = ((), (), s32[]{:S(2)}) async-start(), calls=%async_computation.12 | async-start | bytes 17825792 | tf_op jit(solution)/shard_map/all_gather | solution.py:93
Sparse Core Ops, SparseCore 0:
  27.1 88.8 all-reduce.3
  282.5 47.1 all-gather.6
  332.4 111.2 all-gather.10
  468.7 85.4 all-reduce.5
  721.4 47.1 all-gather.8
  771.1 111.2 all-gather.12
where the time goes:
time: 972 us; the launch traced here: 960 us
  waiting for transfers between devices  473 us (49%)
  other arithmetic  272 us (28%)
  local copies, waits for them, and re-layouts  73.5 us (8%)
  matrix products  64.6 us (7%)
  blocking collectives  51 us (5%)
  between operations  20.1 us (2%)
    all_gather x2, waiting for transfers between devices, per_device(): gathered = lax.all_gather(panel_rows, 'row', axis=0, tiled=True)  220 us
    another operation x29, other arithmetic, block_inverse(): lower_diag = jnp.linalg.cholesky(diagonal)  158 us
    psum x2, waiting for transfers between devices, broadcast(): return lax.psum(kept, axis)  155 us
    all_gather x2, waiting for transfers between devices, broadcast_2(): lax.all_gather(x, axis)  94.5 us
    another operation x5, other arithmetic, block_inverse(): jax.scipy.linalg.solve_triangular(lower_diag, identity_block, lower=True)  80.9 us
    dot_general x2, matrix products, outer_update(): lax.dot_general(left_rows, right_rows, (((1,), (1,)), ((), ())), precisio...  38.3 us
    unnamed x12, local copies, waits for them, and re-layouts  28.3 us
    all_to_all x2, blocking collectives, summed_on_arrival(): tiles = lax.all_to_all(cut_along(x, dim, devices), axis, 0, 0, tiled=True)  25.4 us
  transfers between devices with their start and end apart: 7, of which 7 were waited for; matrix products, arithmetic and copies ran while one was open for 1% of the time, Pallas kernels for 0%

commit v1 on v0

--- a/solution.py
+++ b/solution.py
@@ -90,7 +90,15 @@
         panel_rows = broadcast_2(row_slice, "col", owner_col)
         factor_list.append(panel_rows)
         update_rows = jnp.where(row_block[:, None] > panel_step, panel_rows, 0.0)
-        gathered = lax.all_gather(panel_rows, "row", axis=0, tiled=True)
+        gathered = jnp.concatenate(
+            lax.all_to_all(
+                jnp.stack([panel_rows for _ in range(lax.axis_size("row"))]),
+                axis_name="row",
+                split_axis=0,
+                concat_axis=0,
+            ),
+            0,
+        )
         grouped = gathered.reshape(
             row_groups // col_groups, col_groups, local_blocks, PANEL, slice_width
         )

time: 972 us -> 1280 us (1.32)
  waiting for transfers between devices: 473 us -> 745 us
  local copies, waits for them, and re-layouts: 73.5 us -> 87.9 us
  starting transfers between devices: 5.34 us -> 18.8 us
    all_to_all x0 -> x2, waiting for transfers between devices: none -> 495 us  [per_device(): lax.all_to_all(jnp.stack([panel_rows for _ in range(lax.axis_size('row'))...]
    all_gather x2 -> x0, waiting for transfers between devices: 220 us -> none  [per_device(): gathered = lax.all_gather(panel_rows, 'row', axis=0, tiled=True)]
    another operation x0 -> x2, local copies, waits for them, and re-layouts: none -> 14.6 us  [per_device(): jnp.stack([panel_rows for _ in range(lax.axis_size('row'))])]
    all_to_all x0 -> x2, starting transfers between devices: none -> 13.6 us  [per_device(): lax.all_to_all(jnp.stack([panel_rows for _ in range(lax.axis_size('row'))...]
where the time goes in v1:
time: 1280 us; the launch traced here: 1270 us
  waiting for transfers between devices  745 us (58%)
  other arithmetic  281 us (22%)
  local copies, waits for them, and re-layouts  87.9 us (7%)
  matrix products  64.6 us (5%)
  blocking collectives  53.1 us (4%)
  between operations  19.8 us (2%)
  starting transfers between devices  18.8 us (1%)
    all_to_all x2, waiting for transfers between devices, per_device(): lax.all_to_all(jnp.stack([panel_rows for _ in range(lax.axis_size('row'))...  495 us
    another operation x29, other arithmetic, block_inverse(): lower_diag = jnp.linalg.cholesky(diagonal)  168 us
    psum x2, waiting for transfers between devices, broadcast(): return lax.psum(kept, axis)  153 us
    all_gather x2, waiting for transfers between devices, broadcast_2(): lax.all_gather(x, axis)  94.7 us
    another operation x5, other arithmetic, block_inverse(): jax.scipy.linalg.solve_triangular(lower_diag, identity_block, lower=True)  80.9 us
    dot_general x2, matrix products, outer_update(): lax.dot_general(left_rows, right_rows, (((1,), (1,)), ((), ())), precisio...  38.3 us
    unnamed x12, local copies, waits for them, and re-layouts  28.3 us
    all_to_all x2, blocking collectives, summed_on_arrival(): tiles = lax.all_to_all(cut_along(x, dim, devices), axis, 0, 0, tiled=True)  27.6 us
  transfers between devices with their start and end apart: 7, of which 7 were waited for; matrix products, arithmetic and copies ran while one was open for 1% of the time, Pallas kernels for 0%

profile of v1, /device:TPU:1, one launch (start us, length us, event | category | flops | bytes accessed | tf_op | source)
XLA Modules:
  0.0 1269.8 jit_solution(5869491338663105507)
XLA Ops:
  7.2 17.5 %copy.60 = f32[1,1024,4096]{1,2,0:T(8,128)} copy(f32[1,1024,4096]{2,1,0:T(8,128)} %param.4) | data formatting | bytes 33554432 | tf_op args[0]
  24.7 2.3 slice_select_fusion.1
  27.0 1.7 slice.113
  30.2 5.1 all-to-all-start
  35.4 2.5 all-to-all-done
  39.3 76.7 %all-reduce.4.cloned.1.call-done = f32[512,512]{0,1:T(8,128)} async-done(((f32[512,512]{0,1:T(8,128)}), f32[512,512]{0,1:T(8,128)}) %all-reduce.4.cloned.1.call-update) | async-done | bytes 1048592 | tf_op jit(solution)/shard_map/psum | solution.py:12
  116.0 1.6 copy.63
  117.8 8.2 all_to_all.67
  126.0 1.9 reduce_sum.46
  129.4 11.7 cholesky.286
  141.2 9.8 custom-call.27
  153.6 11.7 cholesky.305
  165.4 10.0 custom-call.28
  177.0 11.7 cholesky.326
  189.4 9.8 custom-call.29
  200.6 21.9 %cholesky.343 = f32[128,128]{1,0:T(8,128)S(1)} custom-call(f32[128,128]{1,0:T(8,128)S(1)} %convolution_subtract_fusion.13), custom_call_target="Cholesky" | custom-call | tf_op jit(solution)/shard_map/jit(cholesky)/cholesky | solution.py:40
  227.7 11.7 while.4
  228.3 2.2 bitcast_dynamic-update-slice_fusion.4
  231.3 2.2 bitcast_dynamic-update-slice_fusion.4
  234.2 2.2 bitcast_dynamic-update-slice_fusion.4
  237.1 2.2 bitcast_dynamic-update-slice_fusion.4
  239.3 39.3 %custom-call.30 = f32[4,128,128]{1,2,0:T(8,128)S(1)} custom-call(f32[4,128,128]{2,1,0:T(8,128)S(1)} %get-tuple-element.18), custom_call_target="InvertDiagBlocksLowerTriangular" | custom-call | tf_op jit(solution)/shard_map/jit(_solve_triangular)/triangular_solve | solution.py:41
  282.5 1.6 convolution_subtract_fusion.7
  284.5 1.9 convolution_select_fusion.1
  286.4 4.6 all_to_all.68
  292.3 47.3 %all-gather.3.cloned.1.call-done = f32[4,1024,256]{2,1,0:T(8,128)} async-done(((f32[1,1024,256]{2,1,0:T(8,128)}), f32[4,1024,256]{2,1,0:T(8,128)}) %all-gather.3.cloned.1.call-update) | async-done | bytes 4194320 | tf_op jit(solution)/shard_map/all_gather | solution.py:36
  339.7 2.3 fusion.96
  342.0 7.3 stack.6
  349.3 6.6 all-to-all-start.3
  356.0 248.1 %all-to-all-done.3 = f32[16,1024,256]{2,1,0:T(8,128)} async-done(((f32[16,1024,256]{2,1,0:T(8,128)}), f32[16,1024,256]{2,1,0:T(8,128)}, u32[]{:S(2)}, u32[]{:S(2)}) %all-to-all-start.3) | async-done | bytes 16777248 | tf_op jit(solution)/shard_map/all_to_all | solution.py:94
  604.2 3.3 bitcast_select_fusion.1
  607.7 19.2 %convolution_subtract_fusion.1 = f32[1024,4096]{0,1:T(8,128)} fusion(f32[4096,256]{1,0:T(8,128)S(1)} %bitcast.147, pred[1024]{0:T(1024)(128)(4,1)S(1)} %broadcast_compare_fusion.2, f32[1,1024,4096]{1,2,0:T(8,128)} %copy.60, f32[4,1024,256]{2,1,0:T(8,128)} %all-gather.3.cloned.1.call-done), kind=kOutput, calls=%fused_computation.6 | convolution fusion | flops 12889358336 | bytes 38798336 | tf_op jit(solution)/shard_map/dot_general | solution.py:45
  626.9 2.5 slice_select_fusion
  629.7 7.0 all_to_all.69
  637.9 75.9 %all-reduce.6.cloned.1.call-done = f32[512,512]{0,1:T(8,128)} async-done(((f32[512,512]{0,1:T(8,128)}), f32[512,512]{0,1:T(8,128)}) %all-reduce.6.cloned.1.call-update) | async-done | bytes 1048592 | tf_op jit(solution)/shard_map/psum | solution.py:12
  713.8 1.6 copy.70
  715.6 8.2 all_to_all.70
  723.8 1.9 reduce_sum.48
  727.2 11.7 cholesky.358
  739.1 9.8 custom-call.31
  751.4 11.7 cholesky.377
  764.5 10.0 custom-call.32
  776.1 11.7 cholesky.398
  788.5 9.8 custom-call.33
  799.8 11.9 cholesky.415
  815.9 11.7 while.5
  816.6 2.2 bitcast_dynamic-update-slice_fusion.5
  819.6 2.2 bitcast_dynamic-update-slice_fusion.5
  822.5 2.2 bitcast_dynamic-update-slice_fusion.5
  825.4 2.2 bitcast_dynamic-update-slice_fusion.5
  827.6 39.3 %custom-call.34 = f32[4,128,128]{1,2,0:T(8,128)S(1)} custom-call(f32[4,128,128]{2,1,0:T(8,128)S(1)} %get-tuple-element.19), custom_call_target="InvertDiagBlocksLowerTriangular" | custom-call | tf_op jit(solution)/shard_map/jit(_solve_triangular)/triangular_solve | solution.py:41
  870.8 1.6 convolution_subtract_fusion.6
  872.8 1.9 convolution_select_fusion
  874.7 4.6 all_to_all.71
  880.6 47.3 %all-gather.5.cloned.1.call-done = f32[4,1024,256]{2,1,0:T(8,128)} async-done(((f32[1,1024,256]{2,1,0:T(8,128)}), f32[4,1024,256]{2,1,0:T(8,128)}) %all-gather.5.cloned.1.call-update) | async-done | bytes 4194320 | tf_op jit(solution)/shard_map/all_gather | solution.py:36
  929.3 7.3 stack.8
  936.6 7.0 all-to-all-start.7
  945.1 246.8 %all-to-all-done.7 = f32[16,1024,256]{2,1,0:T(8,128)} async-done(((f32[16,1024,256]{2,1,0:T(8,128)}), f32[16,1024,256]{2,1,0:T(8,128)}, u32[]{:S(2)}, u32[]{:S(2)}) %all-to-all-start.7) | async-done | bytes 16777248 | tf_op jit(solution)/shard_map/all_to_all | solution.py:94
  1191.9 3.3 bitcast_select_fusion
  1195.5 19.2 %convolution_subtract_fusion = f32[1024,4096]{0,1:T(8,128)} fusion(f32[1024,4096]{0,1:T(8,128)} %convolution_subtract_fusion.1, f32[4096,256]{1,0:T(8,128)S(1)} %bitcast.148, pred[1024]{0:T(1024)(128)(4,1)S(1)} %broadcast_compare_fusion.3, f32[4,1024,256]{2,1,0:T(8,128)} %all-gather.5.cloned.1.call-done), kind=kOutput, calls=%fused_computation.5 | convolution fusion | flops 12889358336 | bytes 38798336 | tf_op jit(solution)/shard_map/dot_general | solution.py:45
  1214.6 6.8 copy.89
  1221.5 20.6 %all_to_all.72 = f32[2,512,4096]{1,2,0:T(8,128)} all-to-all(f32[2,512,4096]{1,2,0:T(8,128)S(1)} %bitcast.146), channel_id=1, replica_groups=mesh['row'=16,'col'=4,'depth'=2] {'depth'}, dimensions={0} | all-to-all | bytes 33554432 | tf_op jit(solution)/shard_map/all_to_all | solution.py:31
  1242.1 11.9 reduce_sum.49
  1254.0 8.9 copy.77
  (112 shorter events, 46.5 us)
Async XLA Ops:
  7.2 108.8 %all-reduce.4.cloned.1.call-start = ((), (), s32[]{:S(2)}) async-start(), calls=%async_computation.9 | async-start | bytes 2097152 | tf_op jit(solution)/shard_map/psum | solution.py:12
  30.2 7.6 all-to-all-start
  35.4 304.3 %all-gather.3.cloned.1.call-start = ((), (), s32[]{:S(2)}) async-start(), calls=%async_computation.10 | async-start | bytes 5242880 | tf_op jit(solution)/shard_map/all_gather | solution.py:36
  128.4 1.0 copy-start.4
  226.5 58.0 %copy-start.1 = (f32[512,512]{0,1:T(8,128)S(1)}, f32[512,512]{0,1:T(8,128)}, u32[]{:S(2)}) copy-start(f32[512,512]{0,1:T(8,128)} %reduce_sum.45) | copy-start | bytes 3145732
  349.3 254.9 %all-to-all-start.3 = ((f32[16,1024,256]{2,1,0:T(8,128)}), f32[16,1024,256]{2,1,0:T(8,128)}, u32[]{:S(2)}, u32[]{:S(2)}) async-start(f32[16,1024,256]{2,1,0:T(8,128)} %stack.6), calls=%async_computation.3 | async-start | bytes 33554432 | tf_op jit(solution)/shard_map/all_to_all | solution.py:94
  355.9 357.9 %all-reduce.6.cloned.1.call-start = ((), (), s32[]{:S(2)}) async-start(), calls=%async_computation.11 | async-start | bytes 2097152 | tf_op jit(solution)/shard_map/psum | solution.py:12
  626.9 2.6 slice-start
  629.4 298.5 %all-gather.5.cloned.1.call-start = ((), (), s32[]{:S(2)}) async-start(), calls=%async_computation.12 | async-start | bytes 5242880 | tf_op jit(solution)/shard_map/all_gather | solution.py:36
  726.2 1.0 copy-start.3
  814.8 58.0 %copy-start.2 = (f32[512,512]{0,1:T(8,128)S(1)}, f32[512,512]{0,1:T(8,128)}, u32[]{:S(2)}) copy-start(f32[512,512]{0,1:T(8,128)} %reduce_sum.47) | copy-start | bytes 3145732
  936.6 7.1 copy-start
  936.6 255.3 %all-to-all-start.7 = ((f32[16,1024,256]{2,1,0:T(8,128)}), f32[16,1024,256]{2,1,0:T(8,128)}, u32[]{:S(2)}, u32[]{:S(2)}) async-start(f32[16,1024,256]{2,1,0:T(8,128)} %stack.8), calls=%async_computation.7 | async-start | bytes 33554432 | tf_op jit(solution)/shard_map/all_to_all | solution.py:94
Sparse Core Ops, SparseCore 0:
  27.1 88.8 all-reduce.3
  292.4 47.1 all-gather.2
  629.5 84.1 all-reduce.5
  880.7 47.1 all-gather.4
